TPU v7x, 32 devices: a whole 2x2x4 slice. The times are simulated.
32 devices in a mesh: patch: 8 (over z, y), hidden: 4 (over x, core).
Axes of the slice: x: 2, y: 2, z: 4, core: 2. Of those that a mesh axis runs over, the one named last changes fastest.
Arguments:
- nodes: bfloat16 [16384, 512], P('patch', 'hidden'), may hold values from -6 to 6
- edges: bfloat16 [65536, 512], P(('patch', 'hidden')), may hold values from -6 to 6
- senders: int32 [65536], P(('patch', 'hidden')), may hold values from 0 to 4159
- receivers: int32 [65536], P(('patch', 'hidden')), may hold values from 0 to 2047
- halo_rows: int32 [8, 2, 1024], P('patch'), may hold values from 0 to 2047
- coarse_rows: int32 [8, 8, 8], P('patch'), may hold values from 0 to 63
- edge_count: int32 [32], P(('patch', 'hidden')), may hold values from 1024 to 2048, as said below
- w_edge_in: bfloat16 [1536, 512], replicated, may hold values from -0.15625 to 0.15625
- b_edge_in: float32 [512], replicated, may hold values from -3 to 3
- w_edge_out: bfloat16 [512, 512], replicated, may hold values from -0.25 to 0.25
- b_edge_out: float32 [512], replicated, may hold values from -2 to 2
- edge_gain: float32 [512], replicated, may hold values from 0.5 to 1.5
- edge_shift: float32 [512], replicated, may hold values from -1 to 1
- w_node_in: bfloat16 [1024, 512], replicated, may hold values from -0.1875 to 0.1875
- b_node_in: float32 [512], replicated, may hold values from -3 to 3
- w_node_out: bfloat16 [512, 512], replicated, may hold values from -0.25 to 0.25
- b_node_out: float32 [512], replicated, may hold values from -2 to 2
- node_gain: float32 [512], replicated, may hold values from 0.5 to 1.5
- node_shift: float32 [512], replicated, may hold values from -1 to 1
Outputs:
- nodes_out: bfloat16 [16384, 512], P('patch', 'hidden')
- edges_out: bfloat16 [65536, 512], P(('patch', 'hidden'))
Inputs may be any that keep to these rules, and one draw needn't show every extreme that they name: `edge_count`: some block holds 2048 live edges.
All inputs are finite; a program needn't handle non-finite values.
Results may differ from a plain program's by a relative error of at most 0.007.
Values may be sent and summed in bfloat16 or wider, within the bound.
A program may use at most 128 MiB of HBM per device.

v0:
```python
import functools

import jax
import jax.numpy as jnp
from jax import lax
from jax.experimental import pallas as pl
from jax.experimental.pallas import tpu as pltpu
from jax.sharding import PartitionSpec as P

layer_epsilon = 1e-05
MESH = pl.DeviceIdType.MESH
f32 = jnp.float32
bf16 = jnp.bfloat16


def normalize(output, norm_gain, norm_shift):
    row_mean = jnp.mean(output, axis=1, keepdims=True)
    centered = output - row_mean
    row_var = jnp.mean(jnp.square(centered), axis=1, keepdims=True)
    return centered * lax.rsqrt(row_var + layer_epsilon) * norm_gain + norm_shift


def silu(value):
    half = 0.5 * value
    return half + half * jnp.tanh(half)


def dot(a, b):
    return jnp.dot(a, b, preferred_element_type=f32)


def column_of(row):
    return jnp.transpose(jnp.broadcast_to(row, (128, row.shape[1])))[:, :1]


def onehot_of(column, start, count):
    ids = lax.broadcasted_iota(jnp.int32, (column.shape[0], count), 1) + start
    return jnp.where(column == ids, 1.0, 0.0).astype(bf16)


def kernel(
    patches, slot, border, block,
    nodes, halo, coarse, live, send_row, recv_row,
    b_ei, b_eo, e_gain, e_shift, b_ni, b_no, n_gain, n_shift,
    edges_hbm, w_ei_hbm, w_eo_hbm, w_ni_hbm, w_no_hbm,
    nodes_out, edges_out,
    table, stage, req, rep, far_in, far_out, send_col, recv_col, edges,
    w_ei, w_eo, w_ni, w_no, pre, own_send, msg,
    give_far, got_far, give_cross, got_cross, give_near, got_near, fresh,
    load_sem, own_sem, store_sem, ag_send, ag_recv, halo_send, halo_recv,
    req_send, req_recv, rep_send, rep_recv, rs_send, rs_recv, out_send, out_recv,
):
    p = lax.axis_index("patch")
    h = lax.axis_index("hidden")
    near = h + 1 - 2 * lax.rem(h, 2)
    cross = lax.rem(h + 2, 4)
    diag = lax.rem(near + 2, 4)
    rows, cols = nodes.shape
    width = edges.shape[1]
    count = edges.shape[0]
    far = patches * slot
    after = lax.rem(p + 1, patches)
    before = lax.rem(p + patches - 1, patches)

    loads = [
        pltpu.make_async_copy(source, target, load_sem.at[i])
        for i, (source, target) in enumerate((
            (edges_hbm, edges), (w_ei_hbm, w_ei), (w_eo_hbm, w_eo), (w_ni_hbm, w_ni),
            (w_no_hbm, w_no),
        ))
    ]
    for load in loads:
        load.start()

    def mine(index):
        return pl.ds(pl.multiple_of(index * cols, cols), cols)

    barrier = pltpu.get_barrier_semaphore()
    for step in range(1, patches):
        pl.semaphore_signal(
            barrier, inc=1, device_id={"patch": lax.rem(p + step, patches)}, device_id_type=MESH
        )
    for peer in (near, cross, diag):
        pl.semaphore_signal(barrier, inc=1, device_id={"hidden": peer}, device_id_type=MESH)
    pl.semaphore_wait(barrier, patches - 1 + 3)

    def remote(source, target, s_sem, r_sem, device):
        return pltpu.make_async_remote_copy(
            src_ref=source, dst_ref=target, send_sem=s_sem, recv_sem=r_sem,
            device_id=device, device_id_type=MESH,
        )

    def slots(index):
        return pl.ds(pl.multiple_of(index * slot, slot), slot)

    asks = []
    for step in range(1, patches):
        owner = lax.rem(p + step, patches)
        ask = remote(
            coarse.at[slots(owner)], req.at[slots(p)],
            req_send.at[step - 1], req_recv.at[step - 1], {"patch": owner},
        )
        ask.start()
        asks.append(ask)

    half = rows // 2
    piece_rows = border // 2
    spans = [(0, half), (half, half)]
    for i in range(2):
        spans.append((rows + i * piece_rows, piece_rows))
        spans.append((rows + border + i * piece_rows, piece_rows))
    spans.append((rows + 2 * border, far))

    def exchange(k, source):
        start, size = spans[k]
        span = pl.ds(start, size)
        pair = []
        for j, peer in ((1, cross), (0, near)):
            copy = remote(
                source, table.at[span, mine(h)], ag_send.at[k, j], ag_recv.at[k, j], {"hidden": peer}
            )
            copy.start()
            pair.append(copy)
        return pair

    def forward(k):
        start, size = spans[k]
        piece = table.at[pl.ds(start, size), mine(cross)]
        copy = remote(piece, piece, ag_send.at[k, 2], ag_recv.at[k, 2], {"hidden": near})
        copy.start()
        return copy

    pairs = [exchange(0, nodes.at[pl.ds(0, half)]), exchange(1, nodes.at[pl.ds(half, half)])]
    keep = pltpu.make_async_copy(nodes, table.at[pl.ds(0, rows), mine(h)], own_sem.at[0])
    keep.start()
    req[slots(p), :] = coarse[slots(p), :]
    pad = table.shape[0] - rows - 2 * border - far
    if pad:
        table[pl.ds(rows + 2 * border + far, pad), :] = jnp.zeros((pad, width), bf16)

    halos = []
    for i in range(2):
        for side, target in ((1, after), (0, before)):
            k = len(halos)
            start, size = spans[2 + k]
            held = pl.ds(k * piece_rows, piece_rows)
            ids = column_of(halo[side : side + 1, i * piece_rows : (i + 1) * piece_rows])
            stage[held, :] = dot(onehot_of(ids, 0, rows), nodes[...]).astype(bf16)
            copy = remote(
                stage.at[held], table.at[pl.ds(start, size), mine(h)],
                halo_send.at[k], halo_recv.at[k], {"patch": target},
            )
            copy.start()
            halos.append(copy)

    for ask in asks:
        ask.wait()
    rep[...] = dot(onehot_of(req[...][:, :1], 0, rows), nodes[...])
    answers = []
    for step in range(1, patches):
        reader = lax.rem(p + step, patches)
        answer = remote(
            rep.at[slots(reader)], far_in.at[slots(p)],
            rep_send.at[step - 1], rep_recv.at[step - 1], {"patch": reader},
        )
        answer.start()
        answers.append(answer)
    far_in[slots(p), :] = rep[slots(p), :]

    keep.wait()
    recv_col[...] = column_of(recv_row[...])
    send_col[...] = column_of(send_row[...])
    for load in loads[:2]:
        load.wait()

    def begin(step, carry):
        part = pl.ds(pl.multiple_of(step * block, block), block)
        pre[part, :] = dot(edges[part, :], w_ei[pl.ds(0, width), :]) + b_ei[...]
        return carry

    lax.fori_loop(0, count // block, begin, 0)

    def relay(k):
        halos[k].wait()
        start, size = spans[2 + k]
        pairs.append(exchange(2 + k, table.at[pl.ds(start, size), mine(h)]))

    relay(0)
    relay(1)
    pairs[0][0].wait()
    forwards = [forward(0)]
    relay(2)
    pairs[1][0].wait()
    forwards.append(forward(1))
    for answer in answers:
        answer.wait()
    far_out[...] = far_in[...].astype(bf16)
    far_pair = exchange(6, far_out)
    keep = pltpu.make_async_copy(
        far_out, table.at[pl.ds(rows + 2 * border, far), mine(h)], own_sem.at[1]
    )
    keep.start()
    for i in range(2):
        pairs[i][1].wait()
        forwards[i].wait()

    def first(step, carry):
        part = pl.ds(pl.multiple_of(step * block, block), block)
        receiver_rows = dot(onehot_of(recv_col[part, :], 0, rows), table[pl.ds(0, rows), :]).astype(bf16)
        own_send[part, :] = dot(
            onehot_of(send_col[part, :], 0, rows), table[pl.ds(0, rows), :]
        ).astype(bf16)
        pre[part, :] = pre[part, :] + dot(receiver_rows, w_ei[pl.ds(2 * width, width), :])
        return carry

    steps = count // block
    lax.fori_loop(0, 1, first, 0)
    relay(3)
    pairs.append(far_pair)
    lax.fori_loop(1, steps - 1, first, 0)
    for k in (2, 3, 4):
        pairs[k][0].wait()
        forwards.append(forward(k))
    lax.fori_loop(steps - 1, steps, first, 0)

    keep.wait()
    for k in (6, 5):
        pairs[k][0].wait()
        forwards.append(forward(k))
    for k in range(2, 7):
        pairs[k][1].wait()
    for copy in forwards[2:]:
        copy.wait()
    for load in loads[2:]:
        load.wait()
    rest = table.shape[0] - rows

    def second(step, carry):
        part = pl.ds(pl.multiple_of(step * block, block), block)
        other = dot(onehot_of(send_col[part, :], rows, rest), table[pl.ds(rows, rest), :])
        sender_rows = (other + own_send[part, :].astype(f32)).astype(bf16)
        active = silu(pre[part, :] + dot(sender_rows, w_ei[pl.ds(width, width), :])).astype(bf16)
        output = dot(active, w_eo[...]) + b_eo[...]
        update = normalize(output, e_gain[...], e_shift[...])
        position = lax.broadcasted_iota(jnp.int32, (block, 1), 0) + step * block
        message = jnp.where(position < live[...], update, 0.0)
        msg[part, :] = message.astype(bf16)
        edges[part, :] = (edges[part, :].astype(f32) + message).astype(bf16)
        return carry

    lax.fori_loop(0, count // block, second, 0)
    save = pltpu.make_async_copy(edges, edges_out, store_sem.at[0])
    save.start()

    share = rows // 4

    def sums(owner):
        ids = lax.broadcasted_iota(jnp.int32, (share, count), 0) + owner * share
        return dot(jnp.where(recv_row[...] == ids, 1.0, 0.0).astype(bf16), msg[...])

    give_far[...] = sums(diag).astype(bf16)
    to_far = remote(give_far, got_far, rs_send.at[0], rs_recv.at[0], {"hidden": near})
    to_far.start()
    pre[pl.ds(0, share), :] = sums(cross)
    to_far.wait()
    cut = share // 4
    to_cross = []
    for i in range(4):
        part = pl.ds(i * cut, cut)
        give_cross[part, :] = (pre[part, :] + got_far[part, :].astype(f32)).astype(bf16)
        copy = remote(
            give_cross.at[part], got_cross.at[part], rs_send.at[1 + i], rs_recv.at[1 + i], {"hidden": cross}
        )
        copy.start()
        to_cross.append(copy)
    give_near[...] = sums(near).astype(bf16)
    to_near = remote(give_near, got_near, rs_send.at[5], rs_recv.at[5], {"hidden": near})
    to_near.start()
    pre[pl.ds(0, share), :] = sums(h)
    own_rows = pl.ds(pl.multiple_of(h * share, share), share)
    pre[pl.ds(share, share), :] = (
        dot(table[own_rows, :], w_ni[pl.ds(0, width), :]) + b_ni[...]
    )
    to_near.wait()
    outs = []
    for i in range(4):
        part = pl.ds(i * cut, cut)
        to_cross[i].wait()
        total = pre[part, :] + got_near[part, :].astype(f32) + got_cross[part, :].astype(f32)
        node_pre = pre[pl.ds(share + i * cut, cut), :] + dot(
            total.astype(bf16), w_ni[pl.ds(width, width), :]
        )
        output = dot(silu(node_pre).astype(bf16), w_no[...]) + b_no[...]
        update = normalize(output, n_gain[...], n_shift[...])
        place = pl.ds(pl.multiple_of(h * share + i * cut, cut), cut)
        fresh[part, :] = (table[place, :].astype(f32) + update).astype(bf16)
        for j, peer in enumerate((cross, diag, near)):
            copy = remote(
                fresh.at[part, mine(peer)], nodes_out.at[place, :],
                out_send.at[i, j], out_recv.at[i, j], {"hidden": peer},
            )
            copy.start()
            outs.append(copy)
        nodes_out[place, :] = fresh[part, mine(h)]
    for copy in outs:
        copy.wait()
    save.wait()


def local(
    nodes, edges, senders, receivers, halo_rows, coarse_rows, edge_count,
    w_edge_in, b_edge_in, w_edge_out, b_edge_out, edge_gain, edge_shift,
    w_node_in, b_node_in, w_node_out, b_node_out, node_gain, node_shift,
    *, patches,
):
    rows, cols = nodes.shape
    count, width = edges.shape
    border = halo_rows.shape[2]
    slot = coarse_rows.shape[2]
    far = patches * slot
    table_rows = -(-(rows + 2 * border + far) // 256) * 256
    share = rows // 4
    block = min(512, count)
    coarse = jnp.broadcast_to(coarse_rows.reshape(far, 1), (far, 128))
    vmem = pl.BlockSpec(memory_space=pltpu.VMEM)
    hbm = pl.BlockSpec(memory_space=pl.ANY)
    dma = pltpu.SemaphoreType.DMA
    return pl.pallas_call(
        functools.partial(kernel, patches, slot, border, block),
        out_shape=(
            jax.ShapeDtypeStruct((rows, cols), bf16),
            jax.ShapeDtypeStruct((count, width), bf16),
        ),
        in_specs=[vmem] * 14 + [hbm] * 5,
        out_specs=(vmem, hbm),
        scratch_shapes=[
            pltpu.VMEM((table_rows, width), bf16),
            pltpu.VMEM((2 * border, cols), bf16),
            pltpu.VMEM((far, 128), jnp.int32),
            pltpu.VMEM((far, cols), f32),
            pltpu.VMEM((far, cols), f32),
            pltpu.VMEM((far, cols), bf16),
            pltpu.VMEM((count, 1), jnp.int32),
            pltpu.VMEM((count, 1), jnp.int32),
            pltpu.VMEM((count, width), bf16),
            pltpu.VMEM(w_edge_in.shape, bf16),
            pltpu.VMEM(w_edge_out.shape, bf16),
            pltpu.VMEM(w_node_in.shape, bf16),
            pltpu.VMEM(w_node_out.shape, bf16),
            pltpu.VMEM((count, width), f32),
            pltpu.VMEM((count, width), bf16),
            pltpu.VMEM((count, width), bf16),
        ] + [pltpu.VMEM((share, width), bf16)] * 7 + [
            dma((5,)), dma((2,)), dma((1,)), dma((7, 3)), dma((7, 3)), dma((4,)), dma((4,)),
            dma((patches - 1,)), dma((patches - 1,)), dma((patches - 1,)), dma((patches - 1,)),
            dma((6,)), dma((6,)), dma((4, 3)), dma((4, 3)),
        ],
        compiler_params=pltpu.CompilerParams(
            collective_id=0, has_side_effects=True, vmem_limit_bytes=60 * 1024 * 1024
        ),
    )(
        nodes, halo_rows.reshape(2, border), coarse, edge_count.reshape(1, 1),
        senders.reshape(1, -1), receivers.reshape(1, -1),
        b_edge_in.reshape(1, -1), b_edge_out.reshape(1, -1),
        edge_gain.reshape(1, -1), edge_shift.reshape(1, -1),
        b_node_in.reshape(1, -1), b_node_out.reshape(1, -1),
        node_gain.reshape(1, -1), node_shift.reshape(1, -1),
        edges,
        w_edge_in, w_edge_out, w_node_in, w_node_out,
    )


def solution(mesh):
    spread = P(("patch", "hidden"))
    return jax.shard_map(
        functools.partial(local, patches=mesh.shape["patch"]),
        mesh=mesh,
        in_specs=(
            P("patch", "hidden"), P(("patch", "hidden"), None), spread, spread,
            P("patch", None, None), P("patch", None, None), spread,
        ) + (P(),) * 12,
        out_specs=(P("patch", "hidden"), P(("patch", "hidden"), None)),
        check_vma=False,
    )
```

profile of v0, /device:TPU:0, one launch (start us, length us, event | category | flops | bytes accessed | tf_op | source)
XLA Modules:
  0.0 75.0 jit_solution(9621308622130150359)
XLA Ops:
  1.3 0.8 %broadcast_in_dim.7 = s32[64]{0:T(128)S(1)} reshape(s32[1,8,8]{2,1,0:T(8,128)} %param.24) | data formatting | bytes 512 | tf_op jit(solution)/shard_map/broadcast_in_dim | solution.py:324
  2.0 0.7 broadcast_in_dim.8.coarse
  2.7 67.4 %shard_map.194 = (bf16[2048,128]{1,0:T(8,128)(2,1)}, bf16[2048,512]{1,0:T(8,128)(2,1)}) custom-call(bf16[2048,128]{1,0:T(8,128)(2,1)} %nodes.1, s32[2,1024]{1,0:T(2,128)} %bitcast.13, s32[64,128]{1,0:T(8,128)} %broadcast_in_dim.8.coarse, s32[1,1]{1,0:T(1,128)} %bitcast.12.live, s32[1,2048]{1,0:T(1,128)} %bitcast.14, s32[1,2048]{1,0:T(1,128)} %bitcast.15, ...), custom_call_target="tpu_custom_call" | custom-call | tf_op jit(solution)/shard_map/pallas_call | solution.py:328
  70.1 1.9 %copy.24 = bf16[2048,128]{1,0:T(8,128)(2,1)} copy(bf16[2048,128]{1,0:T(8,128)(2,1)} %get-tuple-element.4) | data formatting | bytes 1048576
  72.0 3.0 %copy.25 = bf16[2048,512]{1,0:T(8,128)(2,1)} copy(bf16[2048,512]{1,0:T(8,128)(2,1)} %get-tuple-element.5) | data formatting | bytes 4194304
where the time goes:
time: 75.3 us; the launch traced here: 75 us
  Pallas kernels  67.4 us (90%)
  local copies, waits for them, and re-layouts  6.37 us (8%)
  between operations  1.29 us (2%)
    pallas_call x1, Pallas kernels, local(): pl.pallas_call(functools.partial(kernel, patches, slot, border, block), o...  67.4 us
    unnamed x2, local copies, waits for them, and re-layouts  4.91 us

commit v1 on v0

v1 whole, which is shorter than its diff:
```python
import functools

import jax
import jax.numpy as jnp
from jax import lax
from jax.experimental import pallas as pl
from jax.experimental.pallas import tpu as pltpu
from jax.sharding import PartitionSpec as P

layer_epsilon = 1e-05
MESH = pl.DeviceIdType.MESH
f32 = jnp.float32
bf16 = jnp.bfloat16
LANES = 128

PIECES = ((0, 2, "x"), (2, 2, "x"), (4, 1, "x"), (5, 2, "y"), (7, 1, "y"))
NODE_CHUNKS = 4
GATHER = 128


def normalize(output, norm_gain, norm_shift):
    row_mean = jnp.mean(output, axis=1, keepdims=True)
    centered = output - row_mean
    row_var = jnp.mean(jnp.square(centered), axis=1, keepdims=True)
    return centered * lax.rsqrt(row_var + layer_epsilon) * norm_gain + norm_shift


def silu(value):
    half = 0.5 * value
    return half + half * jnp.tanh(half)


def dot(a, b):
    return jnp.dot(a, b, preferred_element_type=f32)


def column_of(row):
    return jnp.transpose(jnp.broadcast_to(row, (LANES, row.shape[1])))[:, :1]


def onehot_of(column, start, count):
    ids = lax.broadcasted_iota(jnp.int32, (column.shape[0], count), 1) + start
    return jnp.where(column == ids, 1.0, 0.0).astype(bf16)


def kernel(
    patches, slot, border, block, quads,
    halo, coarse, live, recv_row,
    b_ei, b_eo, e_gain, e_shift, b_ni, b_no, n_gain, n_shift,
    nodes_hbm, edges_hbm, w_ei_hbm, w_eo_hbm, w_ni_hbm, w_no_hbm, send_hbm, recv_hbm,
    nodes_out, edges,
    table, tab_s, tab_r, got_s, got_r, stage, late_stage, asked, req, rep, far_in, far_out,
    w_ei, w_eo, w_ni, w_no, pre, node_pre, sums_own, msg, send_ids, recv_ids,
    give_far, got_far, give_cross, got_cross, give_near, got_near, fresh,
    load_sem, own_sem, ag_send, ag_recv, halo_send, halo_recv, late_send, late_recv,
    req_send, req_recv, rep_send, rep_recv, rs_send, rs_recv, out_send, out_recv,
):
    p = lax.axis_index("patch")
    h = lax.axis_index("hidden")
    near = h + 1 - 2 * lax.rem(h, 2)
    cross = lax.rem(h + 2, 4)
    diag = lax.rem(near + 2, 4)
    rows, cols = nodes_out.shape
    count, width = edges.shape
    far = patches * slot
    after = lax.rem(p + 1, patches)
    before = lax.rem(p + patches - 1, patches)
    share = rows // 4

    barrier = pltpu.get_barrier_semaphore()
    for step in range(1, patches):
        pl.semaphore_signal(
            barrier, inc=1, device_id={"patch": lax.rem(p + step, patches)}, device_id_type=MESH
        )
    for peer in (near, cross, diag):
        pl.semaphore_signal(barrier, inc=1, device_id={"hidden": peer}, device_id_type=MESH)

    def mine(index):
        return pl.ds(pl.multiple_of(index * cols, cols), cols)

    loads = [
        pltpu.make_async_copy(source, target, load_sem.at[i])
        for i, (source, target) in enumerate((
            (nodes_hbm, table.at[pl.ds(0, rows), mine(h)]),
            (w_ei_hbm, w_ei), (edges_hbm, edges), (recv_hbm, recv_ids), (send_hbm, send_ids),
            (w_ni_hbm, w_ni), (w_eo_hbm, w_eo), (w_no_hbm, w_no),
        ))
    ]
    for load in loads:
        load.start()

    def remote(source, target, s_sem, r_sem, device):
        return pltpu.make_async_remote_copy(
            src_ref=source, dst_ref=target, send_sem=s_sem, recv_sem=r_sem,
            device_id=device, device_id_type=MESH,
        )

    def slots(index):
        return pl.ds(pl.multiple_of(index * slot, slot), slot)

    chunk = rows // NODE_CHUNKS
    spans = [(i * chunk, chunk) for i in range(NODE_CHUNKS)]
    spans.append((rows + 2 * border, far))
    far_span = NODE_CHUNKS
    unit = border // 8
    pieces = []
    for first, units, route in PIECES:
        for side in (1, 0):
            pieces.append((len(spans), side, first * unit, units * unit, route))
            spans.append((rows + (1 - side) * border + first * unit, units * unit))

    def place(k, column):
        start, size = spans[k]
        return table.at[pl.ds(start, size), mine(column)]

    def to_peer(k, j, column, peer, source=None):
        copy = remote(
            place(k, column) if source is None else source, place(k, column),
            ag_send.at[k, j], ag_recv.at[k, j], {"hidden": peer},
        )
        copy.start()
        return copy

    loads[0].wait()
    pl.semaphore_wait(barrier, patches - 1 + 3)

    crossed, neared, passed = {}, {}, {}
    for k in range(NODE_CHUNKS):
        crossed[k] = to_peer(k, 0, h, cross)
        neared[k] = to_peer(k, 1, h, near)

    for owner in range(patches):
        codes = coarse[owner : owner + 1, :].astype(f32)
        square = jnp.broadcast_to(codes, (slot, slot))
        picked = jnp.where(
            lax.broadcasted_iota(jnp.int32, (slot, slot), 0)
            == lax.broadcasted_iota(jnp.int32, (slot, slot), 1), square, 0.0,
        )
        column = jnp.sum(picked, axis=1, keepdims=True)
        asked[pl.ds(owner * slot, slot), :] = jnp.broadcast_to(column, (slot, LANES)).astype(jnp.int32)
    asks = []
    for step in range(1, patches):
        owner = lax.rem(p + step, patches)
        ask = remote(
            asked.at[slots(owner)], req.at[slots(p)],
            req_send.at[step - 1], req_recv.at[step - 1], {"patch": owner},
        )
        ask.start()
        asks.append(ask)
    req[slots(p), :] = asked[slots(p), :]

    def halo_part(side, first, size, column, target):
        ids = column_of(halo[side : side + 1, first : first + size])
        target[...] = dot(onehot_of(ids, 0, rows), table[pl.ds(0, rows), mine(column)]).astype(bf16)

    def halo_copy(source, k, side, column, s_sem, r_sem):
        copy = remote(source, place(k, column), s_sem, r_sem, {"patch": after if side else before})
        copy.start()
        return copy

    halos = {}
    for i, (k, side, first, size, route) in enumerate(pieces):
        held = stage.at[pl.ds(side * border + first, size)]
        halo_part(side, first, size, h, held)
        halos[k] = halo_copy(held, k, side, h, halo_send.at[i], halo_recv.at[i])

    for load in loads[1:3]:
        load.wait()

    def begin(step, carry):
        part = pl.ds(pl.multiple_of(step * block, block), block)
        pre[part, :] = dot(edges[part, :], w_ei[pl.ds(0, width), :]) + b_ei[...]
        return carry

    lax.fori_loop(0, 1, begin, 0)
    for ask in asks:
        ask.wait()
    rep[...] = dot(onehot_of(req[...][:, :1], 0, rows), table[pl.ds(0, rows), mine(h)])
    answers = []
    for step in range(1, patches):
        reader = lax.rem(p + step, patches)
        answer = remote(
            rep.at[slots(reader)], far_in.at[slots(p)],
            rep_send.at[step - 1], rep_recv.at[step - 1], {"patch": reader},
        )
        answer.start()
        answers.append(answer)
    far_in[slots(p), :] = rep[slots(p), :]
    lax.fori_loop(1, count // block, begin, 0)

    def forward(k):
        passed[k] = to_peer(k, 2, cross, near)

    def project(start, size, weight, target):
        projected = dot(table[pl.ds(start, size), :], w_ei[pl.ds(weight * width, width), :])
        for q in range(quads):
            flat = target.reshape(target.shape[0] * quads, LANES)
            flat[pl.ds(start * quads + q, size, stride=quads), :] = (
                projected[:, q * LANES : (q + 1) * LANES]
            )

    def own_chunk(k):
        neared[k].wait()
        passed[k].wait()
        start, size = spans[k]
        project(start, size, 2, tab_r)
        project(start, size, 1, tab_s)

    relayed = [piece for piece in pieces if piece[4] == "x"]
    delayed = [piece for piece in pieces if piece[4] == "y"]

    def relay(piece):
        k = piece[0]
        halos[k].wait()
        if piece[4] == "x":
            crossed[k] = to_peer(k, 0, h, cross)
        neared[k] = to_peer(k, 1, h, near)

    queue = list(relayed)
    for k in range(NODE_CHUNKS):
        crossed[k].wait()
        forward(k)
        if k == 1:
            for answer in answers:
                answer.wait()
            far_out[...] = far_in[...].astype(bf16)
            crossed[far_span] = to_peer(far_span, 0, h, cross, far_out)
            neared[far_span] = to_peer(far_span, 1, h, near, far_out)
            keep = pltpu.make_async_copy(far_out, place(far_span, h), own_sem.at[0])
            keep.start()
        if k == NODE_CHUNKS - 1:
            lates = {}
            for i, (j, side, first, size, route) in enumerate(delayed):
                held = late_stage.at[pl.ds(side * border + first, size)]
                halo_part(side, first, size, cross, held)
                lates[j] = halo_copy(held, j, side, cross, late_send.at[i], late_recv.at[i])
        if k >= 1:
            own_chunk(k - 1)
            for _ in range(2):
                if queue:
                    relay(queue.pop(0))
    while queue:
        relay(queue.pop(0))
    own_chunk(NODE_CHUNKS - 1)
    for piece in delayed:
        relay(piece)
    for load in loads[3:]:
        load.wait()

    def pick(ids, source, target):
        def step(group, carry):
            base = group * GATHER
            for u in range(GATHER):
                target[base + u] = source[ids[base + u]]
            return carry

        lax.fori_loop(0, count // GATHER, step, 0)

    pick(recv_ids, tab_r, got_r)
    own_rows = pl.ds(pl.multiple_of(h * share, share), share)
    node_pre[...] = dot(table[own_rows, :], w_ni[pl.ds(0, width), :]) + b_ni[...]

    keep.wait()
    crossed[far_span].wait()
    forward(far_span)
    for piece in relayed:
        crossed[piece[0]].wait()
        forward(piece[0])
    neared[far_span].wait()
    passed[far_span].wait()
    project(spans[far_span][0], spans[far_span][1], 1, tab_s)
    for piece in relayed:
        k = piece[0]
        neared[k].wait()
        passed[k].wait()
        project(spans[k][0], spans[k][1], 1, tab_s)
    for piece in delayed:
        lates[piece[0]].wait()
        forward(piece[0])
    for piece in delayed:
        k = piece[0]
        neared[k].wait()
        passed[k].wait()
        project(spans[k][0], spans[k][1], 1, tab_s)

    pick(send_ids, tab_s, got_s)

    def edge(step, carry):
        base = pl.multiple_of(step * block, block)
        part = pl.ds(base, block)
        total = [
            pre[part, q * LANES : (q + 1) * LANES]
            + got_r.reshape(count * quads, LANES)[pl.ds(base * quads + q, block, stride=quads), :]
            + got_s.reshape(count * quads, LANES)[pl.ds(base * quads + q, block, stride=quads), :]
            for q in range(quads)
        ]
        active = silu(jnp.concatenate(total, axis=1)).astype(bf16)
        output = dot(active, w_eo[...]) + b_eo[...]
        update = normalize(output, e_gain[...], e_shift[...])
        position = lax.broadcasted_iota(jnp.int32, (block, 1), 0) + step * block
        message = jnp.where(position < live[0], update, 0.0)
        msg[part, :] = message.astype(bf16)
        edges[part, :] = (edges[part, :].astype(f32) + message).astype(bf16)
        return carry

    lax.fori_loop(0, count // block, edge, 0)

    half = share // 2

    def sums(owner, c):
        ids = lax.broadcasted_iota(jnp.int32, (half, count), 0) + (owner * share + c * half)
        return dot(jnp.where(recv_row[...] == ids, 1.0, 0.0).astype(bf16), msg[...])

    to_far, to_near, to_cross = [], [], []
    for c in range(2):
        part = pl.ds(c * half, half)
        give_far[part, :] = sums(diag, c).astype(bf16)
        copy = remote(
            give_far.at[part], got_far.at[part], rs_send.at[c], rs_recv.at[c], {"hidden": near}
        )
        copy.start()
        to_far.append(copy)
    cut = share // 4
    for c in range(2):
        part = pl.ds(c * half, half)
        total = sums(cross, c)
        to_far[c].wait()
        give_cross[part, :] = (total + got_far[part, :].astype(f32)).astype(bf16)
        for i in (2 * c, 2 * c + 1):
            piece = pl.ds(i * cut, cut)
            copy = remote(
                give_cross.at[piece], got_cross.at[piece], rs_send.at[2 + i], rs_recv.at[2 + i],
                {"hidden": cross},
            )
            copy.start()
            to_cross.append(copy)
    for c in range(2):
        part = pl.ds(c * half, half)
        give_near[part, :] = sums(near, c).astype(bf16)
        copy = remote(
            give_near.at[part], got_near.at[part], rs_send.at[6 + c], rs_recv.at[6 + c], {"hidden": near}
        )
        copy.start()
        to_near.append(copy)
    for c in range(2):
        sums_own[pl.ds(c * half, half), :] = sums(h, c)
    for copy in to_near:
        copy.wait()
    outs = []
    for i in range(4):
        part = pl.ds(i * cut, cut)
        to_cross[i].wait()
        total = sums_own[part, :] + got_near[part, :].astype(f32) + got_cross[part, :].astype(f32)
        inner = node_pre[part, :] + dot(total.astype(bf16), w_ni[pl.ds(width, width), :])
        output = dot(silu(inner).astype(bf16), w_no[...]) + b_no[...]
        update = normalize(output, n_gain[...], n_shift[...])
        spot = pl.ds(pl.multiple_of(h * share + i * cut, cut), cut)
        fresh[part, :] = (table[spot, :].astype(f32) + update).astype(bf16)
        for j, peer in enumerate((cross, diag, near)):
            copy = remote(
                fresh.at[part, mine(peer)], nodes_out.at[spot, :],
                out_send.at[i, j], out_recv.at[i, j], {"hidden": peer},
            )
            copy.start()
            outs.append(copy)
        nodes_out[spot, :] = fresh[part, mine(h)]
    for copy in outs:
        copy.wait()


def local(
    nodes, edges, senders, receivers, halo_rows, coarse_rows, edge_count,
    w_edge_in, b_edge_in, w_edge_out, b_edge_out, edge_gain, edge_shift,
    w_node_in, b_node_in, w_node_out, b_node_out, node_gain, node_shift,
    *, patches,
):
    rows, cols = nodes.shape
    count, width = edges.shape
    border = halo_rows.shape[2]
    slot = coarse_rows.shape[2]
    far = patches * slot
    table_rows = rows + 2 * border + far
    share = rows // 4
    block = min(512, count)
    quads = width // LANES
    vmem = pl.BlockSpec(memory_space=pltpu.VMEM)
    smem = pl.BlockSpec(memory_space=pltpu.SMEM)
    hbm = pl.BlockSpec(memory_space=pl.ANY)
    dma = pltpu.SemaphoreType.DMA
    spans = NODE_CHUNKS + 1 + 2 * len(PIECES)
    late = 2 * sum(piece[2] == "y" for piece in PIECES)
    return pl.pallas_call(
        functools.partial(kernel, patches, slot, border, block, quads),
        out_shape=(pltpu.VMEM((rows, cols), bf16), pltpu.VMEM((count, width), bf16)),
        in_specs=[vmem] * 2 + [smem] + [vmem] * 9 + [hbm] * 8,
        out_specs=(vmem, vmem),
        scratch_shapes=[
            pltpu.VMEM((table_rows, width), bf16),
            pltpu.VMEM((table_rows, quads, LANES), f32),
            pltpu.VMEM((rows, quads, LANES), f32),
            pltpu.VMEM((count, quads, LANES), f32),
            pltpu.VMEM((count, quads, LANES), f32),
            pltpu.VMEM((2 * border, cols), bf16),
            pltpu.VMEM((2 * border, cols), bf16),
            pltpu.VMEM((far, LANES), jnp.int32),
            pltpu.VMEM((far, LANES), jnp.int32),
            pltpu.VMEM((far, cols), f32),
            pltpu.VMEM((far, cols), f32),
            pltpu.VMEM((far, cols), bf16),
            pltpu.VMEM(w_edge_in.shape, bf16),
            pltpu.VMEM(w_edge_out.shape, bf16),
            pltpu.VMEM(w_node_in.shape, bf16),
            pltpu.VMEM(w_node_out.shape, bf16),
            pltpu.VMEM((count, width), f32),
            pltpu.VMEM((share, width), f32),
            pltpu.VMEM((share, width), f32),
            pltpu.VMEM((count, width), bf16),
            pltpu.SMEM((count,), jnp.int32),
            pltpu.SMEM((count,), jnp.int32),
        ] + [pltpu.VMEM((share, width), bf16)] * 7 + [
            dma((8,)), dma((1,)), dma((spans, 3)), dma((spans, 3)),
            dma((2 * len(PIECES),)), dma((2 * len(PIECES),)), dma((late,)), dma((late,)),
            dma((patches - 1,)), dma((patches - 1,)), dma((patches - 1,)), dma((patches - 1,)),
            dma((8,)), dma((8,)), dma((4, 3)), dma((4, 3)),
        ],
        compiler_params=pltpu.CompilerParams(
            collective_id=0, has_side_effects=True, vmem_limit_bytes=56 * 1024 * 1024
        ),
    )(
        halo_rows.reshape(2, border), coarse_rows.reshape(patches, slot), edge_count,
        receivers.reshape(1, -1),
        b_edge_in.reshape(1, -1), b_edge_out.reshape(1, -1),
        edge_gain.reshape(1, -1), edge_shift.reshape(1, -1),
        b_node_in.reshape(1, -1), b_node_out.reshape(1, -1),
        node_gain.reshape(1, -1), node_shift.reshape(1, -1),
        nodes, edges, w_edge_in, w_edge_out, w_node_in, w_node_out, senders, receivers,
    )


def solution(mesh):
    spread = P(("patch", "hidden"))
    return jax.shard_map(
        functools.partial(local, patches=mesh.shape["patch"]),
        mesh=mesh,
        in_specs=(
            P("patch", "hidden"), P(("patch", "hidden"), None), spread, spread,
            P("patch", None, None), P("patch", None, None), spread,
        ) + (P(),) * 12,
        out_specs=(P("patch", "hidden"), P(("patch", "hidden"), None)),
        check_vma=False,
    )
```

time: 75.3 us -> 66.5 us (0.88)
  Pallas kernels: 67.4 us -> 63 us
  local copies, waits for them, and re-layouts: 6.37 us -> 2.11 us
    pallas_call x1, Pallas kernels: 67.4 us -> 63 us  [local(): pl.pallas_call(functools.partial(kernel, patches, slot, border, block, qu...]
    unnamed x2, local copies, waits for them, and re-layouts: 4.91 us -> 2.11 us
    broadcast_in_dim x2 -> x0, local copies, waits for them, and re-layouts: 1.46 us -> none  [local(): coarse = jnp.broadcast_to(coarse_rows.reshape(far, 1), (far, 128))]
where the time goes in v1:
time: 66.5 us; the launch traced here: 66.4 us
  Pallas kernels  63 us (95%)
  local copies, waits for them, and re-layouts  2.11 us (3%)
  between operations  1.29 us (2%)
    pallas_call x1, Pallas kernels, local(): pl.pallas_call(functools.partial(kernel, patches, slot, border, block, qu...  63 us
    unnamed x2, local copies, waits for them, and re-layouts  2.11 us

profile of v1, /device:TPU:0, one launch (start us, length us, event | category | flops | bytes accessed | tf_op | source)
XLA Modules:
  0.0 66.4 jit_solution(9074686816061609776)
XLA Ops:
  1.3 63.0 %shard_map.194 = (bf16[2048,128]{1,0:T(8,128)(2,1)S(1)}, bf16[2048,512]{1,0:T(8,128)(2,1)S(1)}) custom-call(s32[2,1024]{1,0:T(2,128)} %bitcast.12, s32[8,8]{1,0:T(8,128)} %bitcast.13, s32[1]{0:T(128)S(6)} %copy.25.live, s32[1,2048]{1,0:T(1,128)} %bitcast.11, f32[1,512]{1,0:T(1,128)} %bitcast.14, f32[1,512]{1,0:T(1,128)} %bitcast.15, f32[1,512]{1,0:T(1,128)} %bitcast.16, ...), custom_call_target="tpu_custom_call" | custom-call | tf_op jit(solution)/shard_map/pallas_call | solution.py:392
  64.2 0.8 %copy.23 = bf16[2048,128]{1,0:T(8,128)(2,1)} copy(bf16[2048,128]{1,0:T(8,128)(2,1)S(1)} %get-tuple-element.2) | data formatting | bytes 1048576
  65.0 1.3 %copy.24 = bf16[2048,512]{1,0:T(8,128)(2,1)} copy(bf16[2048,512]{1,0:T(8,128)(2,1)S(1)} %get-tuple-element.3) | data formatting | bytes 4194304

commit v2 on v1

v2 whole, which is shorter than its diff:
```python
import functools

import jax
import jax.numpy as jnp
from jax import lax
from jax.experimental import pallas as pl
from jax.experimental.pallas import tpu as pltpu
from jax.sharding import PartitionSpec as P

layer_epsilon = 1e-05
MESH = pl.DeviceIdType.MESH
f32 = jnp.float32
bf16 = jnp.bfloat16
LANES = 128

PIECES = ((0, 2, "x"), (2, 2, "x"), (4, 1, "x"), (5, 1, "y"), (6, 2, "y"))
NODE_CHUNKS = 4
GATHER = 128
STORE_PARTS = 4


def normalize(output, norm_gain, norm_shift):
    row_mean = jnp.mean(output, axis=1, keepdims=True)
    centered = output - row_mean
    row_var = jnp.mean(jnp.square(centered), axis=1, keepdims=True)
    return centered * lax.rsqrt(row_var + layer_epsilon) * norm_gain + norm_shift


def silu_of_half(half):
    return half + half * jnp.tanh(half)


def dot(a, b):
    return jnp.dot(a, b, preferred_element_type=f32)


def onehot_of(column, start, count):
    ids = lax.broadcasted_iota(jnp.int32, (column.shape[0], count), 1) + start
    return jnp.where(column == ids, 1.0, 0.0).astype(bf16)


def kernel(
    patches, slot, border, block, quads,
    nodes_hbm, halo_hbm, coarse_hbm, edges_hbm, w_ei_hbm, w_eo_hbm, w_ni_hbm, w_no_hbm,
    send_hbm, recv_hbm, recv_row_hbm, live_hbm, *rest,
):
    vectors_hbm = rest[:8]
    (
        nodes_out, edges,
        table, tab_s, tab_r, got_s0, got_s1, got_r, plain, picked_rows, stage, late_stage,
        coarse, asked, req, rep, far_in, far_out, recv_row, vectors,
        w_ei, w_eo, w_ni, w_no, pre, node_pre, sums_own, msg,
        send_ids, recv_ids, halo_ids, live,
        give_far, got_far, give_cross, got_cross, give_near, got_near, fresh,
        load_sem, own_sem, ag_send, cross_recv, pass_recv, halo_send, halo_recv, late_send, late_recv,
        ask_sem, rs_send, rs_recv, out_sem,
    ) = rest[8:]
    got_s = (got_s0, got_s1)
    b_ei, b_eo, e_gain, e_shift, b_ni, b_no, n_gain, n_shift = [vectors.at[i] for i in range(8)]
    p = lax.axis_index("patch")
    h = lax.axis_index("hidden")
    near = h + 1 - 2 * lax.rem(h, 2)
    cross = lax.rem(h + 2, 4)
    diag = lax.rem(near + 2, 4)
    rows, cols = nodes_out.shape
    count, width = edges.shape
    far = patches * slot
    after = lax.rem(p + 1, patches)
    before = lax.rem(p + patches - 1, patches)
    share = rows // 4

    barrier = pltpu.get_barrier_semaphore()
    for step in range(1, patches):
        pl.semaphore_signal(
            barrier, inc=1, device_id={"patch": lax.rem(p + step, patches)}, device_id_type=MESH
        )
    for peer in (near, cross, diag):
        pl.semaphore_signal(barrier, inc=1, device_id={"hidden": peer}, device_id_type=MESH)

    def mine(index):
        return pl.ds(pl.multiple_of(index * cols, cols), cols)

    def load(i, *pairs):
        copies = [pltpu.make_async_copy(source, target, load_sem.at[i]) for source, target in pairs]
        for copy in copies:
            copy.start()
        return copies[0]

    load_nodes = load(0, (nodes_hbm, table.at[pl.ds(0, rows), mine(h)]))
    border_ids = [halo_ids.at[pl.ds(side * border, border)] for side in range(2)]
    load_halo = [load((11, 1)[side], (halo_hbm.at[side], border_ids[side])) for side in range(2)]
    load_coarse = load(2, (coarse_hbm, coarse))
    load_edges = load(3, (edges_hbm, edges))
    load_in = load(4, (w_ei_hbm, w_ei))
    load(5, *[(source, vectors.at[i]) for i, source in enumerate(vectors_hbm)])
    load_recv = load(6, (recv_hbm, recv_ids))
    load_send = load(7, (send_hbm, send_ids))
    load_row = load(8, (recv_row_hbm, recv_row))
    load_live = load(9, (live_hbm, live))
    load(10, (w_ni_hbm, w_ni), (w_eo_hbm, w_eo), (w_no_hbm, w_no))

    def remote(source, target, s_sem, r_sem, device):
        return pltpu.make_async_remote_copy(
            src_ref=source, dst_ref=target, send_sem=s_sem, recv_sem=r_sem,
            device_id=device, device_id_type=MESH,
        )

    def slots(index):
        return pl.ds(pl.multiple_of(index * slot, slot), slot)

    def drain(sem, blocks, sent=False):
        ref = table.at[pl.ds(0, blocks // quads)]
        total = remote(ref, ref, sem, sem, {"hidden": near})
        if sent:
            total.wait_send()
        else:
            total.wait_recv()

    chunk = rows // NODE_CHUNKS
    spans = [(i * chunk, chunk) for i in range(NODE_CHUNKS)]
    spans.append((rows + 2 * border, far))
    far_span = NODE_CHUNKS
    unit = border // 8
    pieces = []
    for first, units, route in PIECES:
        for side in (1, 0):
            pieces.append((len(spans), side, first * unit, units * unit, route))
            spans.append((rows + (1 - side) * border + first * unit, units * unit))
    early_group, late_group = NODE_CHUNKS, NODE_CHUNKS + 1
    group = {k: k for k in range(NODE_CHUNKS)}
    group[far_span] = late_group
    for k, side, first, size, route in pieces:
        group[k] = early_group if first + size <= border // 2 else late_group
    sent_rows = [0, 0]
    group_rows = [0] * (NODE_CHUNKS + 2)

    def place(k, column):
        start, size = spans[k]
        return table.at[pl.ds(start, size), mine(column)]

    def to_peer(k, j, column, peer, source=None):
        kind = 0 if k < NODE_CHUNKS else 1
        sent_rows[kind] += spans[k][1]
        if j:
            group_rows[group[k]] += spans[k][1]
        copy = remote(
            place(k, column) if source is None else source, place(k, column),
            ag_send.at[kind], pass_recv.at[group[k]] if j else cross_recv.at[k], {"hidden": peer},
        )
        copy.start()
        return copy

    load_nodes.wait()
    pl.semaphore_wait(barrier, patches - 1 + 3)

    crossed = {}
    for k in range(NODE_CHUNKS):
        crossed[k] = to_peer(k, 0, h, cross)
        to_peer(k, 1, h, near)

    load_coarse.wait()
    for owner in range(patches):
        codes = coarse[owner : owner + 1, :].astype(f32)
        square = jnp.broadcast_to(codes, (slot, slot))
        picked = jnp.where(
            lax.broadcasted_iota(jnp.int32, (slot, slot), 0)
            == lax.broadcasted_iota(jnp.int32, (slot, slot), 1), square, 0.0,
        )
        column = jnp.sum(picked, axis=1, keepdims=True)
        asked[pl.ds(owner * slot, slot), :] = jnp.broadcast_to(column, (slot, LANES)).astype(jnp.int32)
    for step in range(1, patches):
        owner = lax.rem(p + step, patches)
        remote(
            asked.at[slots(owner)], req.at[slots(p)], ask_sem.at[0], ask_sem.at[1], {"patch": owner}
        ).start()
    req[slots(p), :] = asked[slots(p), :]
    others = pl.ds(0, (patches - 1) * slot)

    def spread(column):
        plain.reshape(rows, LANES)[...] = table[pl.ds(0, rows), mine(column)].astype(f32)

    def choose(first, size):
        def step(part, carry):
            base = first + part * GATHER
            for u in range(GATHER):
                picked_rows[base + u] = plain[halo_ids[base + u]]
            return carry

        lax.fori_loop(0, size // GATHER, step, 0)

    def halo_part(target, side, first, size):
        start = side * border + first
        choose(start, size)
        part = pl.ds(start, size)
        target[part, :] = picked_rows.reshape(2 * border, LANES)[part, :].astype(bf16)
        return target.at[part]

    def halo_copy(source, k, side, column, s_sem, r_sem):
        copy = remote(source, place(k, column), s_sem, r_sem, {"patch": after if side else before})
        copy.start()
        return copy

    relayed = [piece for piece in pieces if piece[4] == "x"]
    delayed = [piece for piece in pieces if piece[4] == "y"]
    for side in range(2):
        load_halo[side].wait()
    spread(h)
    halos = {}

    def send_halo(i, piece):
        k, side, first, size, route = piece
        held = halo_part(stage, side, first, size)
        halos[k] = halo_copy(held, k, side, h, halo_send.at[0], halo_recv.at[min(i, len(relayed))])

    for i, piece in enumerate(relayed):
        send_halo(i, piece)
    asks = remote(asked.at[others], req.at[others], ask_sem.at[0], ask_sem.at[1], {"hidden": near})
    asks.wait()
    rep[...] = dot(onehot_of(req[...][:, :1], 0, rows), table[pl.ds(0, rows), mine(h)])
    for step in range(1, patches):
        reader = lax.rem(p + step, patches)
        remote(
            rep.at[slots(reader)], far_in.at[slots(p)], ask_sem.at[2], ask_sem.at[3], {"patch": reader}
        ).start()
    answers = remote(rep.at[others], far_in.at[others], ask_sem.at[2], ask_sem.at[3], {"hidden": near})
    far_in[slots(p), :] = rep[slots(p), :]
    for i, piece in enumerate(delayed):
        send_halo(len(relayed) + i, piece)

    load_edges.wait()
    load_in.wait()
    remote(vectors, vectors, load_sem.at[5], load_sem.at[5], {"hidden": near}).wait_recv()

    def begin(step, carry):
        part = pl.ds(pl.multiple_of(step * block, block), block)
        pre[part, :] = 0.5 * (dot(edges[part, :], w_ei[pl.ds(0, width), :]) + b_ei[...])
        return carry

    lax.fori_loop(0, count // block, begin, 0)

    def forward(k):
        to_peer(k, 2, cross, near)

    def project(start, size, weight, target):
        projected = 0.5 * dot(table[pl.ds(start, size), :], w_ei[pl.ds(weight * width, width), :])
        flat = target.reshape(target.shape[0] * quads, LANES)
        for q in range(quads):
            flat[pl.ds(start * quads + q, size, stride=quads), :] = (
                projected[:, q * LANES : (q + 1) * LANES]
            )

    def own_chunk(k):
        drain(pass_recv.at[k], group_rows[k])
        start, size = spans[k]
        project(start, size, 2, tab_r)
        project(start, size, 1, tab_s)

    def relay(piece):
        k = piece[0]
        halos[k].wait_recv()
        crossed[k] = to_peer(k, 0, h, cross)
        to_peer(k, 1, h, near)

    queue = list(relayed)
    for k in range(NODE_CHUNKS):
        crossed[k].wait_recv()
        forward(k)
        if k == NODE_CHUNKS - 1:
            while queue:
                relay(queue.pop(0))
            spread(cross)
            lates = []
            for i, (j, side, first, size, route) in enumerate(delayed):
                held = halo_part(late_stage, side, first, size)
                lates.append((j, halo_copy(held, j, side, cross, late_send.at[0], late_recv.at[i])))
            answers.wait()
            far_out[...] = far_in[...].astype(bf16)
            crossed[far_span] = to_peer(far_span, 0, h, cross, far_out)
            to_peer(far_span, 1, h, near, far_out)
            keep = pltpu.make_async_copy(far_out, place(far_span, h), own_sem.at[0])
            keep.start()
        if k >= 1:
            for _ in range(2):
                if queue:
                    relay(queue.pop(0))
            own_chunk(k - 1)
    own_chunk(NODE_CHUNKS - 1)
    late_rows = sum(piece[3] for piece in delayed)
    drain(halo_recv.at[len(relayed)], late_rows)
    for piece in delayed:
        to_peer(piece[0], 1, h, near)
    load_recv.wait()
    load_send.wait()

    def pick_receivers(start, size):
        def step(part, carry):
            base = start + part * GATHER
            for u in range(GATHER):
                got_r[base + u] = tab_r[recv_ids[base + u]]
            return carry

        lax.fori_loop(0, size // GATHER, step, 0)

    early = [piece for piece in relayed if group[piece[0]] == early_group]
    parts = max(1, len(early) // 2)
    keep.wait()
    for i in range(parts):
        pick_receivers(i * (count // parts), count // parts)
        for piece in early[2 * i : 2 * i + 2]:
            crossed[piece[0]].wait_recv()
            forward(piece[0])

    def merge(step, carry):
        part = pl.ds(pl.multiple_of(step * block, block), block)
        wide = got_r.reshape(count * quads, LANES)
        for q in range(quads):
            lanes = pl.ds(q * LANES, LANES)
            pre[part, lanes] = (
                pre[part, lanes] + wide[pl.ds(step * block * quads + q, block, stride=quads), :]
            )
        return carry

    lax.fori_loop(0, count // block, merge, 0)
    drain(load_sem.at[10], 4 * width * quads)
    own_rows = pl.ds(pl.multiple_of(h * share, share), share)
    node_pre[...] = dot(table[own_rows, :], w_ni[pl.ds(0, width), :]) + b_ni[...]
    drain(pass_recv.at[early_group], group_rows[early_group])
    for side in range(2):
        project(rows + side * border, border // 2, 1, tab_s)
    for piece in relayed:
        if group[piece[0]] == late_group:
            crossed[piece[0]].wait_recv()
            forward(piece[0])
    crossed[far_span].wait_recv()
    forward(far_span)
    for j, copy in lates:
        copy.wait_recv()
        forward(j)
    drain(pass_recv.at[late_group], group_rows[late_group])
    project(spans[far_span][0], spans[far_span][1], 1, tab_s)
    for side in range(2):
        project(rows + side * border + border // 2, border // 2, 1, tab_s)
    load_live.wait()
    load_row.wait()

    def pick_block(index, first, size):
        for u in range(first, first + size):
            got_s[index % 2][u] = tab_s[send_ids[index * block + u]]

    def pick_first(step, carry):
        for u in range(GATHER):
            got_s[0][step * GATHER + u] = tab_s[send_ids[step * GATHER + u]]
        return carry

    def edge(index):
        part = pl.ds(index * block, block)
        wide_s = got_s[index % 2].reshape(block * quads, LANES)
        total = [
            pre[part, q * LANES : (q + 1) * LANES]
            + wide_s[pl.ds(q, block, stride=quads), :]
            for q in range(quads)
        ]
        active = silu_of_half(jnp.concatenate(total, axis=1)).astype(bf16)
        output = dot(active, w_eo[...]) + b_eo[...]
        update = normalize(output, e_gain[...], e_shift[...])
        position = lax.broadcasted_iota(jnp.int32, (block, 1), 0) + index * block
        message = jnp.where(position < live[0], update, 0.0)
        msg[part, :] = message.astype(bf16)
        edges[part, :] = (edges[part, :].astype(f32) + message).astype(bf16)

    lax.fori_loop(0, block // GATHER, pick_first, 0)
    for index in range(count // block):
        if index + 1 < count // block:
            pick_block(index + 1, 0, block)
        edge(index)

    cut = share // 4

    def sums(owner, first, size):
        ids = lax.broadcasted_iota(jnp.int32, (size, count), 0) + (owner * share + first)
        return dot(jnp.where(recv_row[...] == ids, 1.0, 0.0).astype(bf16), msg[...])

    def give_sums(owner, first, size, target, source, r_sem):
        part = pl.ds(first, size)
        source[part, :] = sums(owner, first, size).astype(bf16)
        copy = remote(source.at[part], target.at[part], rs_send.at[0], r_sem, {"hidden": near})
        copy.start()
        return copy

    to_cross = []

    def cross_sums(first, size, copy):
        part = pl.ds(first, size)
        total = sums(cross, first, size)
        copy.wait_recv()
        give_cross[part, :] = (total + got_far[part, :].astype(f32)).astype(bf16)
        for i in range(first // cut, (first + size) // cut):
            piece = pl.ds(i * cut, cut)
            copy = remote(
                give_cross.at[piece], got_cross.at[piece], rs_send.at[0], rs_recv.at[4 + i],
                {"hidden": cross},
            )
            copy.start()
            to_cross.append(copy)

    parts = ((0, cut), (cut, cut), (2 * cut, share - 2 * cut))
    begun = [
        give_sums(diag, *parts[i], got_far, give_far, rs_recv.at[i]) for i in range(2)
    ]
    cross_sums(*parts[0], begun[0])
    cross_sums(*parts[1], begun[1])
    begun.append(give_sums(diag, *parts[2], got_far, give_far, rs_recv.at[2]))
    cross_sums(*parts[2], begun[2])
    to_near = give_sums(near, 0, share, got_near, give_near, rs_recv.at[3])
    sums_own[...] = sums(h, 0, share)
    to_near.wait_recv()
    for i in range(4):
        part = pl.ds(i * cut, cut)
        to_cross[i].wait_recv()
        total = sums_own[part, :] + got_near[part, :].astype(f32) + got_cross[part, :].astype(f32)
        inner = node_pre[part, :] + dot(total.astype(bf16), w_ni[pl.ds(width, width), :])
        output = dot(silu_of_half(0.5 * inner).astype(bf16), w_no[...]) + b_no[...]
        update = normalize(output, n_gain[...], n_shift[...])
        spot = pl.ds(pl.multiple_of(h * share + i * cut, cut), cut)
        fresh[part, :] = (table[spot, :].astype(f32) + update).astype(bf16)
        for peer in (cross, diag, near):
            remote(
                fresh.at[part, mine(peer)], nodes_out.at[spot, :],
                out_sem.at[0], out_sem.at[1], {"hidden": peer},
            ).start()
        nodes_out[spot, :] = fresh[part, mine(h)]
    for kind in range(2):
        drain(ag_send.at[kind], sent_rows[kind], True)
    drain(halo_send.at[0], 2 * border, True)
    drain(late_send.at[0], late_rows, True)
    drain(rs_send.at[0], 3 * share * quads, True)
    drain(out_sem.at[0], 3 * share, True)
    drain(out_sem.at[1], 3 * share)


def store(nodes, edges, nodes_out, edges_out, sems):
    size = edges.shape[0] // STORE_PARTS
    copies = [
        pltpu.make_async_copy(
            edges.at[pl.ds(i * size, size)], edges_out.at[pl.ds(i * size, size)], sems.at[i]
        )
        for i in range(STORE_PARTS)
    ]
    copies.append(pltpu.make_async_copy(nodes, nodes_out, sems.at[STORE_PARTS]))
    for copy in copies:
        copy.start()
    for copy in copies:
        copy.wait()


def local(
    nodes, edges, senders, receivers, halo_rows, coarse_rows, edge_count,
    w_edge_in, b_edge_in, w_edge_out, b_edge_out, edge_gain, edge_shift,
    w_node_in, b_node_in, w_node_out, b_node_out, node_gain, node_shift,
    *, patches,
):
    rows, cols = nodes.shape
    count, width = edges.shape
    border = halo_rows.shape[2]
    slot = coarse_rows.shape[2]
    far = patches * slot
    table_rows = rows + 2 * border + far
    share = rows // 4
    block = min(512, count)
    quads = width // LANES
    vmem = pl.BlockSpec(memory_space=pltpu.VMEM)
    hbm = pl.BlockSpec(memory_space=pl.ANY)
    dma = pltpu.SemaphoreType.DMA
    spans = NODE_CHUNKS + 1 + 2 * len(PIECES)
    late = 2 * sum(piece[2] == "y" for piece in PIECES)
    i32 = jnp.int32
    fresh_nodes, fresh_edges = pl.pallas_call(
        functools.partial(kernel, patches, slot, border, block, quads),
        out_shape=(pltpu.VMEM((rows, cols), bf16), pltpu.VMEM((count, width), bf16)),
        in_specs=[hbm] * 20,
        out_specs=(vmem, vmem),
        scratch_shapes=[
            pltpu.VMEM((table_rows, width), bf16),
            pltpu.VMEM((table_rows, quads, LANES), f32),
            pltpu.VMEM((rows, quads, LANES), f32),
            pltpu.VMEM((block, quads, LANES), f32),
            pltpu.VMEM((block, quads, LANES), f32),
            pltpu.VMEM((count, quads, LANES), f32),
            pltpu.VMEM((rows, 1, LANES), f32),
            pltpu.VMEM((2 * border, 1, LANES), f32),
            pltpu.VMEM((2 * border, cols), bf16),
            pltpu.VMEM((2 * border, cols), bf16),
            pltpu.VMEM((patches, slot), i32),
            pltpu.VMEM((far, LANES), i32),
            pltpu.VMEM((far, LANES), i32),
            pltpu.VMEM((far, cols), f32),
            pltpu.VMEM((far, cols), f32),
            pltpu.VMEM((far, cols), bf16),
            pltpu.VMEM((1, count), i32),
            pltpu.VMEM((8, 1, width), f32),
            pltpu.VMEM(w_edge_in.shape, bf16),
            pltpu.VMEM(w_edge_out.shape, bf16),
            pltpu.VMEM(w_node_in.shape, bf16),
            pltpu.VMEM(w_node_out.shape, bf16),
            pltpu.VMEM((count, width), f32),
            pltpu.VMEM((share, width), f32),
            pltpu.VMEM((share, width), f32),
            pltpu.VMEM((count, width), bf16),
            pltpu.SMEM((count,), i32),
            pltpu.SMEM((count,), i32),
            pltpu.SMEM((2 * border,), i32),
            pltpu.SMEM((1,), i32),
        ] + [pltpu.VMEM((share, width), bf16)] * 7 + [
            dma((12,)), dma((1,)), dma((2,)), dma((spans - late,)), dma((NODE_CHUNKS + 2,)),
            dma((1,)), dma((2 * len(PIECES) - late + 1,)), dma((1,)), dma((late,)),
            dma((4,)), dma((1,)), dma((8,)), dma((2,)),
        ],
        compiler_params=pltpu.CompilerParams(
            collective_id=0, has_side_effects=True, vmem_limit_bytes=56 * 1024 * 1024
        ),
    )(
        nodes, halo_rows.reshape(2, border), coarse_rows.reshape(patches, slot),
        edges, w_edge_in, w_edge_out, w_node_in, w_node_out, senders, receivers,
        receivers.reshape(1, -1), edge_count,
        b_edge_in.reshape(1, -1), b_edge_out.reshape(1, -1),
        edge_gain.reshape(1, -1), edge_shift.reshape(1, -1),
        b_node_in.reshape(1, -1), b_node_out.reshape(1, -1),
        node_gain.reshape(1, -1), node_shift.reshape(1, -1),
    )
    return pl.pallas_call(
        store,
        out_shape=(
            jax.ShapeDtypeStruct((rows, cols), bf16), jax.ShapeDtypeStruct((count, width), bf16)
        ),
        in_specs=[vmem] * 2,
        out_specs=(hbm, hbm),
        scratch_shapes=[dma((1 + STORE_PARTS,))],
    )(
        pltpu.with_memory_space_constraint(fresh_nodes, pltpu.VMEM),
        pltpu.with_memory_space_constraint(fresh_edges, pltpu.VMEM),
    )


def solution(mesh):
    spread = P(("patch", "hidden"))
    return jax.shard_map(
        functools.partial(local, patches=mesh.shape["patch"]),
        mesh=mesh,
        in_specs=(
            P("patch", "hidden"), P(("patch", "hidden"), None), spread, spread,
            P("patch", None, None), P("patch", None, None), spread,
        ) + (P(),) * 12,
        out_specs=(P("patch", "hidden"), P(("patch", "hidden"), None)),
        check_vma=False,
    )
```

time: 66.5 us -> 57.3 us (0.86)
  Pallas kernels: 63 us -> 55.7 us
  local copies, waits for them, and re-layouts: 2.11 us -> 0 us
    pallas_call x1, Pallas kernels: 63 us -> 54.2 us  [local(): pl.pallas_call(functools.partial(kernel, patches, slot, border, block, qu...]
    unnamed x2 -> x0, local copies, waits for them, and re-layouts: 2.11 us -> none
    pallas_call x0 -> x1, Pallas kernels: none -> 1.53 us  [local(): pl.pallas_call(store, out_shape=(jax.ShapeDtypeStruct((rows, cols), bf16)...]
where the time goes in v2:
time: 57.3 us; the launch traced here: 57.2 us
  Pallas kernels  55.7 us (97%)
  between operations  1.45 us (3%)
    pallas_call x1, Pallas kernels, local(): pl.pallas_call(functools.partial(kernel, patches, slot, border, block, qu...  54.2 us
    pallas_call x1, Pallas kernels, local(): pl.pallas_call(store, out_shape=(jax.ShapeDtypeStruct((rows, cols), bf16)...  1.53 us

profile of v2, /device:TPU:0, one launch (start us, length us, event | category | flops | bytes accessed | tf_op | source)
XLA Modules:
  0.0 57.2 jit_solution(3549512823484430092)
XLA Ops:
  1.3 54.2 %shard_map.194 = (bf16[2048,128]{1,0:T(8,128)(2,1)S(1)}, bf16[2048,512]{1,0:T(8,128)(2,1)S(1)}) custom-call(bf16[2048,128]{1,0:T(8,128)(2,1)} %nodes_hbm.1, s32[2,1024]{1,0:T(2,128)} %bitcast.12, s32[8,8]{1,0:T(8,128)} %bitcast.13, bf16[2048,512]{1,0:T(8,128)(2,1)} %edges_hbm.1, bf16[1536,512]{1,0:T(8,128)(2,1)} %w_ei_hbm.1, bf16[512,512]{1,0:T(8,128)(2,1)} %w_eo_hbm.1, ...), custom_call_target="tpu_custom_call" | custom-call | tf_op jit(solution)/shard_map/pallas_call | solution.py:477
  55.5 1.5 %shard_map.195 = (bf16[2048,128]{1,0:T(8,128)(2,1)}, bf16[2048,512]{1,0:T(8,128)(2,1)}) custom-call(bf16[2048,128]{1,0:T(8,128)(2,1)S(1)} %get-tuple-element.4.nodes, bf16[2048,512]{1,0:T(8,128)(2,1)S(1)} %get-tuple-element.5.edges), custom_call_target="tpu_custom_call" | custom-call | tf_op jit(solution)/shard_map/pallas_call | solution.py:530

commit v3 on v2

--- a/solution.py
+++ b/solution.py
@@ -13,7 +13,7 @@
 bf16 = jnp.bfloat16
 LANES = 128
 
-PIECES = ((0, 2, "x"), (2, 2, "x"), (4, 1, "x"), (5, 1, "y"), (6, 2, "y"))
+PIECES = ((0, 2, "x"), (2, 2, "x"), (4, 2, "y"), (6, 2, "y"))
 NODE_CHUNKS = 4
 GATHER = 128
 STORE_PARTS = 4
@@ -322,11 +322,6 @@
 
     lax.fori_loop(0, count // block, merge, 0)
     drain(load_sem.at[10], 4 * width * quads)
-    own_rows = pl.ds(pl.multiple_of(h * share, share), share)
-    node_pre[...] = dot(table[own_rows, :], w_ni[pl.ds(0, width), :]) + b_ni[...]
-    drain(pass_recv.at[early_group], group_rows[early_group])
-    for side in range(2):
-        project(rows + side * border, border // 2, 1, tab_s)
     for piece in relayed:
         if group[piece[0]] == late_group:
             crossed[piece[0]].wait_recv()
@@ -336,6 +331,9 @@
     for j, copy in lates:
         copy.wait_recv()
         forward(j)
+    drain(pass_recv.at[early_group], group_rows[early_group])
+    for side in range(2):
+        project(rows + side * border, border // 2, 1, tab_s)
     drain(pass_recv.at[late_group], group_rows[late_group])
     project(spans[far_span][0], spans[far_span][1], 1, tab_s)
     for side in range(2):
@@ -368,17 +366,18 @@
         msg[part, :] = message.astype(bf16)
         edges[part, :] = (edges[part, :].astype(f32) + message).astype(bf16)
 
-    lax.fori_loop(0, block // GATHER, pick_first, 0)
-    for index in range(count // block):
-        if index + 1 < count // block:
-            pick_block(index + 1, 0, block)
-        edge(index)
-
     cut = share // 4
+    blocks = count // block
 
     def sums(owner, first, size):
         ids = lax.broadcasted_iota(jnp.int32, (size, count), 0) + (owner * share + first)
         return dot(jnp.where(recv_row[...] == ids, 1.0, 0.0).astype(bf16), msg[...])
+
+    lax.fori_loop(0, block // GATHER, pick_first, 0)
+    for index in range(blocks):
+        if index + 1 < blocks:
+            pick_block(index + 1, 0, block)
+        edge(index)
 
     def give_sums(owner, first, size, target, source, r_sem):
         part = pl.ds(first, size)
@@ -403,16 +402,16 @@
             copy.start()
             to_cross.append(copy)
 
-    parts = ((0, cut), (cut, cut), (2 * cut, share - 2 * cut))
-    begun = [
-        give_sums(diag, *parts[i], got_far, give_far, rs_recv.at[i]) for i in range(2)
-    ]
-    cross_sums(*parts[0], begun[0])
-    cross_sums(*parts[1], begun[1])
-    begun.append(give_sums(diag, *parts[2], got_far, give_far, rs_recv.at[2]))
-    cross_sums(*parts[2], begun[2])
+    shares = ((0, cut), (cut, cut), (2 * cut, share - 2 * cut))
+    begun = [give_sums(diag, *shares[i], got_far, give_far, rs_recv.at[i]) for i in range(2)]
+    cross_sums(*shares[0], begun[0])
+    cross_sums(*shares[1], begun[1])
+    begun.append(give_sums(diag, *shares[2], got_far, give_far, rs_recv.at[2]))
+    cross_sums(*shares[2], begun[2])
     to_near = give_sums(near, 0, share, got_near, give_near, rs_recv.at[3])
     sums_own[...] = sums(h, 0, share)
+    own_rows = pl.ds(pl.multiple_of(h * share, share), share)
+    node_pre[...] = dot(table[own_rows, :], w_ni[pl.ds(0, width), :]) + b_ni[...]
     to_near.wait_recv()
     for i in range(4):
         part = pl.ds(i * cut, cut)

time: 57.3 us -> 55.5 us (0.969)
  Pallas kernels: 55.7 us -> 53.9 us
    pallas_call x1, Pallas kernels: 54.2 us -> 52.4 us  [local(): pl.pallas_call(functools.partial(kernel, patches, slot, border, block, qu...]
where the time goes in v3:
time: 55.5 us; the launch traced here: 55.4 us
  Pallas kernels  53.9 us (97%)
  between operations  1.45 us (3%)
    pallas_call x1, Pallas kernels, local(): pl.pallas_call(functools.partial(kernel, patches, slot, border, block, qu...  52.4 us
    pallas_call x1, Pallas kernels, local(): pl.pallas_call(store, out_shape=(jax.ShapeDtypeStruct((rows, cols), bf16)...  1.53 us

profile of v3, /device:TPU:0, one launch (start us, length us, event | category | flops | bytes accessed | tf_op | source)
XLA Modules:
  0.0 55.4 jit_solution(3953282479251109487)
XLA Ops:
  1.3 52.4 %shard_map.194 = (bf16[2048,128]{1,0:T(8,128)(2,1)S(1)}, bf16[2048,512]{1,0:T(8,128)(2,1)S(1)}) custom-call(bf16[2048,128]{1,0:T(8,128)(2,1)} %nodes_hbm.1, s32[2,1024]{1,0:T(2,128)} %bitcast.12, s32[8,8]{1,0:T(8,128)} %bitcast.13, bf16[2048,512]{1,0:T(8,128)(2,1)} %edges_hbm.1, bf16[1536,512]{1,0:T(8,128)(2,1)} %w_ei_hbm.1, bf16[512,512]{1,0:T(8,128)(2,1)} %w_eo_hbm.1, ...), custom_call_target="tpu_custom_call" | custom-call | tf_op jit(solution)/shard_map/pallas_call | solution.py:476
  53.7 1.5 %shard_map.195 = (bf16[2048,128]{1,0:T(8,128)(2,1)}, bf16[2048,512]{1,0:T(8,128)(2,1)}) custom-call(bf16[2048,128]{1,0:T(8,128)(2,1)S(1)} %get-tuple-element.4.nodes, bf16[2048,512]{1,0:T(8,128)(2,1)S(1)} %get-tuple-element.5.edges), custom_call_target="tpu_custom_call" | custom-call | tf_op jit(solution)/shard_map/pallas_call | solution.py:529
